TPU v7x, 32 devices: a whole 2x2x4 slice. The times are simulated.
32 devices in a mesh: ep: 4 (over y, x), grp: 8 (over z, core).
Axes of the slice: x: 2, y: 2, z: 4, core: 2. Of those that a mesh axis runs over, the one named last changes fastest.
Arguments:
- tokens: bfloat16 [4096, 4096], P(('ep', 'grp')), may hold values from -6 to 6
- expert_ids: int32 [4096, 8], P(('ep', 'grp')), may hold values from 0 to 127, all different within a row; in each aligned block of 128 rows (0 to 127, 128 to 255, ...) at most 16 rows name the same one
- combine: float32 [4096, 8], P(('ep', 'grp')), may hold values from 0.05 to 1
- w_gate: bfloat16 [4096, 1280], P(None, 'ep'), may hold values from -0.09375 to 0.09375
- w_up: bfloat16 [4096, 1280], P(None, 'ep'), may hold values from -0.09375 to 0.09375
- w_down: bfloat16 [1280, 4096], P('ep'), may hold values from -0.15625 to 0.15625
- bias: float32 [128], replicated, may hold values from -3 to 3
Outputs:
- mixed: bfloat16 [4096, 4096], P(('ep', 'grp'))
- new_bias: float32 [128], replicated
Inputs may be any that keep to these rules, and one draw needn't show every extreme that they name: `expert_ids`: each row names 8 different experts. Among the rows of one device no expert is named more than 16 times, a bound that some block reaches.
All inputs are finite; a program needn't handle non-finite values.
Results may differ from a plain program's by a relative error of at most 0.0057.
Values may be sent and summed in bfloat16 or wider, within the bound.
A program may use at most 64 MiB of HBM per device.

v0:
```python
import jax
import jax.numpy as jnp
from jax import lax
from jax.sharding import PartitionSpec as P

NEXP = 128
TOPK = 8
SPLIT = 4


def count_loads(expert_ids):
    experts = jnp.arange(NEXP, dtype=jnp.int32)
    local = jnp.sum(
        (expert_ids.reshape(-1)[:, None] == experts[None, :]).astype(jnp.float32), axis=0
    )
    within = lax.psum(local, "ep")
    return lax.psum(within, "grp")


def per_device(tokens, expert_ids, combine, w_gate, w_up, w_down, bias):
    n_ep = lax.axis_size("ep")
    n_grp = lax.axis_size("grp")
    tok_rows = tokens.shape[0]
    width = tokens.shape[1]
    capacity = tok_rows // 8
    win_experts = n_ep // SPLIT
    flat_ids = expert_ids.reshape(-1)
    window = jnp.arange(win_experts, dtype=jnp.int32)
    hit = (flat_ids[:, None] == window[None, :]).astype(jnp.int32)
    ranks = jnp.cumsum(hit, axis=0) - 1
    slot = jnp.sum(hit * ranks, axis=1)
    inside = jnp.sum(hit, axis=1)
    dest = jnp.where(inside > 0, flat_ids * capacity + slot, win_experts * capacity)
    slot_ids = jnp.arange(win_experts * capacity, dtype=jnp.int32)
    chosen = (slot_ids[:, None] == dest[None, :]).reshape(win_experts * capacity, tok_rows, TOPK)
    select = jnp.sum(chosen.astype(jnp.float32), axis=2)
    weights = jnp.sum(chosen.astype(jnp.float32) * combine[None, :, :], axis=2)
    buffer = jnp.dot(
        select.astype(jnp.bfloat16), tokens, preferred_element_type=jnp.float32
    ).astype(jnp.bfloat16)
    outgoing = jnp.repeat(buffer.reshape(win_experts, capacity, width), SPLIT, axis=0)
    block = lax.all_to_all(outgoing, "ep", split_axis=0, concat_axis=0, tiled=True)
    rows = block.reshape(-1, width)
    gate = jnp.dot(rows, w_gate, preferred_element_type=jnp.float32)
    upval = jnp.dot(rows, w_up, preferred_element_type=jnp.float32)
    hidden = (jax.nn.silu(gate) * upval).astype(jnp.bfloat16)
    part = jnp.dot(hidden, w_down, preferred_element_type=jnp.float32).astype(jnp.bfloat16)
    returned = lax.all_to_all(
        part.reshape(block.shape), "ep", split_axis=0, concat_axis=0, tiled=True
    )
    summed = jnp.sum(
        returned.astype(jnp.float32).reshape(win_experts, SPLIT, capacity, width), axis=1
    )
    summed = summed.reshape(win_experts * capacity, width)
    mixed = jnp.dot(
        weights.T, summed, precision=lax.Precision.HIGHEST, preferred_element_type=jnp.float32
    ).astype(jnp.bfloat16)
    load = count_loads(expert_ids)
    mean_load = jnp.float32(tok_rows * n_ep * n_grp * TOPK / NEXP)
    new_bias = bias - 0.05 * (load - mean_load) / jnp.sqrt(mean_load)
    return (mixed, new_bias)


def solution(mesh):
    return jax.shard_map(
        per_device,
        mesh=mesh,
        in_specs=(
            P(("ep", "grp"), None),
            P(("ep", "grp"), None),
            P(("ep", "grp"), None),
            P(None, "ep"),
            P(None, "ep"),
            P("ep", None),
            P(),
        ),
        out_specs=(P(("ep", "grp"), None), P()),
        check_vma=False,
    )
```

profile of v0, /device:TPU:0, one launch (start us, length us, event | category | flops | bytes accessed | tf_op | source)
XLA Modules:
  0.0 56.3 jit_solution(11772067957491407302)
XLA Ops:
  0.6 0.8 %fusion.8 = s32[128,8]{0,1:T(8,128)S(1)} fusion(s32[128,8]{0,1:T(8,128)} %param.8), kind=kLoop, calls=%fused_computation.21 | loop fusion | flops 2048 | bytes 8192 | tf_op jit(solution)/shard_map/convert_element_type | solution.py:29
  1.5 0.1 copy.30
  1.6 0.1 reshape.124
  1.7 0.3 reduce-window.6
  2.0 0.2 slice_reduce_fusion
  2.2 0.1 reshape.117
  2.2 0.2 reduce-window.9
  2.4 0.1 broadcast.76
  2.5 0.1 reshape.120
  2.7 0.9 %add_select_fusion = s32[128,8]{0,1:T(8,128)S(1)} fusion(s32[128,8]{0,1:T(8,128)S(1)} %copy.31, s32[128,8]{0,1:T(8,128)S(1)} %copy.32, s32[128,8]{0,1:T(8,128)} %param.8), kind=kLoop, calls=%fused_computation.18 | loop fusion | flops 9216 | bytes 16384 | tf_op jit(solution)/shard_map/jit(_where)/select_n | solution.py:33
  3.6 0.7 %convert_reduce_fusion.2 = (bf16[16,128]{1,0:T(8,128)(2,1)S(1)}, f32[16,128]{1,0:T(8,128)S(1)}) fusion(s32[128,8]{0,1:T(8,128)S(1)} %add_select_fusion, f32[128,8]{0,1:T(8,128)} %param.9), kind=kLoop, calls=%fused_computation.13 | loop fusion | flops 77824 | bytes 20480 | tf_op jit(solution)/shard_map/reduce_sum | solution.py:36
  4.3 1.5 %convolution_convert_fusion.2 = bf16[16,4096]{1,0:T(8,128)(2,1)S(1)} fusion(bf16[128,4096]{1,0:T(8,128)(2,1)} %param.7, bf16[16,128]{1,0:T(8,128)(2,1)S(1)} %get-tuple-element.2), kind=kOutput, calls=%fused_computation.2 | convolution fusion | flops 16842752 | bytes 1183744 | tf_op jit(solution)/shard_map/dot_general | solution.py:38
  5.8 13.5 %all_to_all.10 = bf16[4,16,4096]{2,1,0:T(8,128)(2,1)S(1)} all-to-all(bf16[4,16,4096]{2,1,0:T(8,128)(2,1)S(1)} %reshape.121), channel_id=1, replica_groups=mesh['ep'=4,'grp'=8] {'ep'}, dimensions={0} | all-to-all | bytes 1048576 | tf_op jit(solution)/shard_map/all_to_all | solution.py:42
  19.3 0.9 %fusion.10 = f32[64,320]{1,0:T(8,128)S(1)} fusion(bf16[64,4096]{1,0:T(8,128)(2,1)S(1)} %bitcast.16, bf16[4096,320]{0,1:T(8,128)(2,1)S(1)} %copy-done.1), kind=kOutput, calls=%fused_computation.25 | convolution fusion | flops 167772160 | bytes 3227648 | tf_op jit(solution)/shard_map/dot_general | solution.py:44
  20.3 4.7 %convolution_convert_fusion.1 = bf16[64,4096]{1,0:T(8,128)(2,1)} fusion(bf16[320,4096]{1,0:T(8,128)(2,1)S(1)} %copy-done, bf16[64,4096]{1,0:T(8,128)(2,1)S(1)} %bitcast.17, bf16[4096,320]{0,1:T(8,128)(2,1)} %param.11, f32[64,320]{1,0:T(8,128)S(1)} %fusion.10), kind=kOutput, calls=%fused_computation.1 | convolution fusion | flops 335929344 | bytes 6373376 | tf_op jit(solution)/shard_map/dot_general | solution.py:47
  25.0 3.5 %all-to-all-start.1 = ((bf16[4,16,4096]{2,1,0:T(8,128)(2,1)}), bf16[4,16,4096]{2,1,0:T(8,128)(2,1)S(1)}, u32[]{:S(2)}, u32[]{:S(2)}) async-start(bf16[4,16,4096]{2,1,0:T(8,128)(2,1)} %bitcast.18), calls=%async_computation.1 | async-start | bytes 1048576 | tf_op jit(solution)/shard_map/all_to_all | solution.py:48
  28.5 0.1 copy.33
  28.6 0.1 eq.58
  28.7 0.2 convert_reduce_fusion.1
  28.9 10.4 %psum.14 = f32[128]{0:T(128)S(1)} all-reduce(f32[128]{0:T(128)S(1)} %convert_reduce_fusion.1), channel_id=1, replica_groups=mesh['ep'=4,'grp'=8] {'ep'}, use_global_device_ids=true, to_apply=%region_6.7 | all-reduce | flops 128 | bytes 1024 | tf_op jit(solution)/shard_map/psum | solution.py:16
  39.3 13.6 %psum.15 = f32[128]{0:T(128)S(1)} all-reduce(f32[128]{0:T(128)S(1)} %psum.14), channel_id=1, replica_groups=mesh['ep'=4,'grp'=8] {'grp'}, use_global_device_ids=true, to_apply=%region_7.8 | all-reduce | flops 128 | bytes 1024 | tf_op jit(solution)/shard_map/psum | solution.py:17
  52.9 0.5 multiply_subtract_fusion
  53.4 0.1 convert_reduce_fusion
  53.5 2.8 %convolution_convert_fusion = bf16[128,4096]{1,0:T(8,128)(2,1)} fusion(f32[16,128]{1,0:T(8,128)S(1)} %get-tuple-element.3, f32[16,4096]{1,0:T(8,128)S(1)} %convert_reduce_fusion), kind=kOutput, calls=%fused_computation | convolution fusion | flops 101187584 | bytes 1318912 | tf_op jit(solution)/shard_map/dot_general | solution.py:55
  (13 shorter events, 0.2 us)
Async XLA Ops:
  0.6 19.6 %copy-start = (bf16[320,4096]{1,0:T(8,128)(2,1)S(1)}, bf16[320,4096]{1,0:T(8,128)(2,1)}, u32[]{:S(2)}) copy-start(bf16[320,4096]{1,0:T(8,128)(2,1)} %param.12) | copy-start | bytes 7864324
  2.7 16.6 %copy-start.1 = (bf16[4096,320]{0,1:T(8,128)(2,1)S(1)}, bf16[4096,320]{0,1:T(8,128)(2,1)}, u32[]{:S(2)}) copy-start(bf16[4096,320]{0,1:T(8,128)(2,1)} %param.10) | copy-start | bytes 7864324
  20.2 8.2 %copy-start.2 = (s32[128,8]{0,1:T(8,128)S(1)}, s32[128,8]{0,1:T(8,128)}, u32[]{:S(2)}) copy-start(s32[128,8]{0,1:T(8,128)} %param.8) | copy-start | bytes 12292
  20.3 32.6 %copy-start.3 = (f32[128]{0:T(128)S(1)}, f32[128]{0:T(128)}, u32[]{:S(2)}) copy-start(f32[128]{0:T(128)} %param.13) | copy-start | bytes 1540
  25.0 28.4 %all-to-all-start.1 = ((bf16[4,16,4096]{2,1,0:T(8,128)(2,1)}), bf16[4,16,4096]{2,1,0:T(8,128)(2,1)S(1)}, u32[]{:S(2)}, u32[]{:S(2)}) async-start(bf16[4,16,4096]{2,1,0:T(8,128)(2,1)} %bitcast.18), calls=%async_computation.1 | async-start | bytes 1048576 | tf_op jit(solution)/shard_map/all_to_all | solution.py:48
where the time goes:
time: 56.6 us; the launch traced here: 56.3 us
  blocking collectives  37.5 us (66%)
  matrix products  9.9 us (17%)
  other arithmetic  3.71 us (7%)
  starting transfers between devices  3.47 us (6%)
  local copies, waits for them, and re-layouts  1 us (2%)
  between operations  0.72 us (1%)
    psum x1, blocking collectives, count_loads(): return lax.psum(within, 'grp')  13.6 us
    all_to_all x1, blocking collectives, per_device(): lax.all_to_all(outgoing, 'ep', split_axis=0, concat_axis=0, tiled=True)  13.5 us
    psum x1, blocking collectives, count_loads(): within = lax.psum(local, 'ep')  10.4 us
    dot_general x1, matrix products, per_device(): jnp.dot(hidden, w_down, preferred_element_type=jnp.float32)  4.74 us
    all_to_all x1, starting transfers between devices, per_device(): lax.all_to_all(part.reshape(block.shape), 'ep', split_axis=0, concat_axis...  3.47 us
    dot_general x1, matrix products, per_device(): jnp.dot(weights.T, summed, precision=lax.Precision.HIGHEST, preferred_ele...  2.81 us
    dot_general x1, matrix products, per_device(): jnp.dot(select.astype(jnp.bfloat16), tokens, preferred_element_type=jnp.f...  1.47 us
  transfers between devices with their start and end apart: 1, of which 0 were waited for; matrix products, arithmetic and copies ran while one was open for 2% of the time, Pallas kernels for 0%

commit v1 on v0

--- a/solution.py
+++ b/solution.py
@@ -13,7 +13,9 @@
     local = jnp.sum(
         (expert_ids.reshape(-1)[:, None] == experts[None, :]).astype(jnp.float32), axis=0
     )
-    within = lax.psum(local, "ep")
+    within = local
+    for hop in (1, 2):
+        within = within + lax.ppermute(within, "ep", [(dev, dev ^ hop) for dev in range(4)])
     return lax.psum(within, "grp")
 
 

time: 56.6 us -> 56.3 us (level)
  blocking collectives: 37.5 us -> 27.1 us
  waiting for transfers between devices: 0.01 us -> 6.56 us
  starting transfers between devices: 3.47 us -> 6.98 us
    psum x1 -> x0, blocking collectives: 10.4 us -> none  [count_loads(): within = lax.psum(local, 'ep')]
    ppermute x0 -> x2, waiting for transfers between devices: none -> 6.56 us  [count_loads(): lax.ppermute(within, 'ep', [(dev, dev ^ hop) for dev in range(4)])]
    ppermute x0 -> x2, starting transfers between devices: none -> 3.51 us  [count_loads(): lax.ppermute(within, 'ep', [(dev, dev ^ hop) for dev in range(4)])]
  transfers between devices with their start and end apart: 1 -> 3, of which waited for: 0 -> 2; matrix products, arithmetic and copies ran while one was open for 2% -> 2% of each run, Pallas kernels for 0% -> 0%
where the time goes in v1:
time: 56.3 us; the launch traced here: 56 us
  blocking collectives  27.1 us (48%)
  matrix products  9.9 us (18%)
  starting transfers between devices  6.98 us (12%)
  waiting for transfers between devices  6.56 us (12%)
  other arithmetic  3.71 us (7%)
  local copies, waits for them, and re-layouts  1 us (2%)
  between operations  0.73 us (1%)
    psum x1, blocking collectives, count_loads(): return lax.psum(within, 'grp')  13.6 us
    all_to_all x1, blocking collectives, per_device(): lax.all_to_all(outgoing, 'ep', split_axis=0, concat_axis=0, tiled=True)  13.5 us
    ppermute x2, waiting for transfers between devices, count_loads(): lax.ppermute(within, 'ep', [(dev, dev ^ hop) for dev in range(4)])  6.56 us
    dot_general x1, matrix products, per_device(): jnp.dot(hidden, w_down, preferred_element_type=jnp.float32)  4.74 us
    ppermute x2, starting transfers between devices, count_loads(): lax.ppermute(within, 'ep', [(dev, dev ^ hop) for dev in range(4)])  3.51 us
    all_to_all x1, starting transfers between devices, per_device(): lax.all_to_all(part.reshape(block.shape), 'ep', split_axis=0, concat_axis...  3.47 us
    dot_general x1, matrix products, per_device(): jnp.dot(weights.T, summed, precision=lax.Precision.HIGHEST, preferred_ele...  2.81 us
    dot_general x1, matrix products, per_device(): jnp.dot(select.astype(jnp.bfloat16), tokens, preferred_element_type=jnp.f...  1.47 us
  transfers between devices with their start and end apart: 3, of which 2 were waited for; matrix products, arithmetic and copies ran while one was open for 2% of the time, Pallas kernels for 0%

profile of v1, /device:TPU:0, one launch (start us, length us, event | category | flops | bytes accessed | tf_op | source)
XLA Modules:
  0.0 56.0 jit_solution(4033066797920190463)
XLA Ops:
  0.6 0.8 %fusion.8 = s32[128,8]{0,1:T(8,128)S(1)} fusion(s32[128,8]{0,1:T(8,128)} %param.8), kind=kLoop, calls=%fused_computation.21 | loop fusion | flops 2048 | bytes 8192 | tf_op jit(solution)/shard_map/convert_element_type | solution.py:31
  1.5 0.1 copy.30
  1.6 0.1 reshape.124
  1.7 0.3 reduce-window.6
  2.0 0.2 slice_reduce_fusion
  2.2 0.2 reduce-window.9
  2.5 0.1 reshape.120
  2.7 0.9 %add_select_fusion = s32[128,8]{0,1:T(8,128)S(1)} fusion(s32[128,8]{0,1:T(8,128)S(1)} %copy.31, s32[128,8]{0,1:T(8,128)S(1)} %copy.32, s32[128,8]{0,1:T(8,128)} %param.8), kind=kLoop, calls=%fused_computation.18 | loop fusion | flops 9216 | bytes 16384 | tf_op jit(solution)/shard_map/jit(_where)/select_n | solution.py:35
  3.6 0.7 %convert_reduce_fusion.2 = (bf16[16,128]{1,0:T(8,128)(2,1)S(1)}, f32[16,128]{1,0:T(8,128)S(1)}) fusion(s32[128,8]{0,1:T(8,128)S(1)} %add_select_fusion, f32[128,8]{0,1:T(8,128)} %param.9), kind=kLoop, calls=%fused_computation.13 | loop fusion | flops 77824 | bytes 20480 | tf_op jit(solution)/shard_map/reduce_sum | solution.py:38
  4.3 1.5 %convolution_convert_fusion.2 = bf16[16,4096]{1,0:T(8,128)(2,1)S(1)} fusion(bf16[128,4096]{1,0:T(8,128)(2,1)} %param.7, bf16[16,128]{1,0:T(8,128)(2,1)S(1)} %get-tuple-element.2), kind=kOutput, calls=%fused_computation.2 | convolution fusion | flops 16842752 | bytes 1183744 | tf_op jit(solution)/shard_map/dot_general | solution.py:40
  5.8 13.5 %all_to_all.10 = bf16[4,16,4096]{2,1,0:T(8,128)(2,1)S(1)} all-to-all(bf16[4,16,4096]{2,1,0:T(8,128)(2,1)S(1)} %reshape.121), channel_id=1, replica_groups=mesh['ep'=4,'grp'=8] {'ep'}, dimensions={0} | all-to-all | bytes 1048576 | tf_op jit(solution)/shard_map/all_to_all | solution.py:44
  19.3 0.9 %fusion.10 = f32[64,320]{1,0:T(8,128)S(1)} fusion(bf16[64,4096]{1,0:T(8,128)(2,1)S(1)} %bitcast.16, bf16[4096,320]{0,1:T(8,128)(2,1)S(1)} %copy-done.1), kind=kOutput, calls=%fused_computation.25 | convolution fusion | flops 167772160 | bytes 3227648 | tf_op jit(solution)/shard_map/dot_general | solution.py:46
  20.3 4.7 %convolution_convert_fusion.1 = bf16[64,4096]{1,0:T(8,128)(2,1)} fusion(bf16[320,4096]{1,0:T(8,128)(2,1)S(1)} %copy-done, bf16[64,4096]{1,0:T(8,128)(2,1)S(1)} %bitcast.17, bf16[4096,320]{0,1:T(8,128)(2,1)} %param.11, f32[64,320]{1,0:T(8,128)S(1)} %fusion.10), kind=kOutput, calls=%fused_computation.1 | convolution fusion | flops 335929344 | bytes 6373376 | tf_op jit(solution)/shard_map/dot_general | solution.py:49
  25.0 3.5 %all-to-all-start.1 = ((bf16[4,16,4096]{2,1,0:T(8,128)(2,1)}), bf16[4,16,4096]{2,1,0:T(8,128)(2,1)S(1)}, u32[]{:S(2)}, u32[]{:S(2)}) async-start(bf16[4,16,4096]{2,1,0:T(8,128)(2,1)} %bitcast.18), calls=%async_computation.1 | async-start | bytes 1048576 | tf_op jit(solution)/shard_map/all_to_all | solution.py:50
  28.5 0.1 copy.33
  28.6 0.1 eq.58
  28.7 0.2 convert_reduce_fusion.1
  28.9 2.0 %collective-permute-start = (f32[128]{0:T(128)S(1)}, f32[128]{0:T(128)S(1)}, u32[]{:S(2)}, u32[]{:S(2)}) collective-permute-start(f32[128]{0:T(128)S(1)} %convert_reduce_fusion.1), channel_id=1, source_target_pairs={{0,8},{8,0},{16,24},{24,16},{1,9},{9,1},{17,25},{25,17},{2,10},{10... | collective-permute-start | bytes 1544 | tf_op jit(solution)/shard_map/ppermute | solution.py:18
  31.0 4.5 %collective-permute-done = f32[128]{0:T(128)S(1)} collective-permute-done((f32[128]{0:T(128)S(1)}, f32[128]{0:T(128)S(1)}, u32[]{:S(2)}, u32[]{:S(2)}) %collective-permute-start) | collective-permute-done | bytes 544 | tf_op jit(solution)/shard_map/ppermute | solution.py:18
  35.4 1.5 %collective-permute-start.1 = (f32[128]{0:T(128)S(1)}, f32[128]{0:T(128)S(1)}, u32[]{:S(2)}, u32[]{:S(2)}) collective-permute-start(f32[128]{0:T(128)S(1)} %add.30), channel_id=1, source_target_pairs={{0,16},{8,24},{16,0},{24,8},{1,17},{9,25},{17,1},{25,9},{2,18},{10... | collective-permute-start | bytes 1544 | tf_op jit(solution)/shard_map/ppermute | solution.py:18
  36.9 2.1 %collective-permute-done.1 = f32[128]{0:T(128)S(1)} collective-permute-done((f32[128]{0:T(128)S(1)}, f32[128]{0:T(128)S(1)}, u32[]{:S(2)}, u32[]{:S(2)}) %collective-permute-start.1) | collective-permute-done | bytes 544 | tf_op jit(solution)/shard_map/ppermute | solution.py:18
  39.0 13.6 %psum.7 = f32[128]{0:T(128)S(1)} all-reduce(f32[128]{0:T(128)S(1)} %add.31), channel_id=1, replica_groups=mesh['ep'=4,'grp'=8] {'grp'}, use_global_device_ids=true, to_apply=%region_6.7 | all-reduce | flops 128 | bytes 1024 | tf_op jit(solution)/shard_map/psum | solution.py:19
  52.6 0.5 multiply_subtract_fusion
  53.2 2.8 %convolution_convert_fusion = bf16[128,4096]{1,0:T(8,128)(2,1)} fusion(f32[16,128]{1,0:T(8,128)S(1)} %get-tuple-element.3, f32[16,4096]{1,0:T(8,128)S(1)} %convert_reduce_fusion), kind=kOutput, calls=%fused_computation | convolution fusion | flops 101187584 | bytes 1318912 | tf_op jit(solution)/shard_map/dot_general | solution.py:57
  (18 shorter events, 0.4 us)
Async XLA Ops:
  0.6 19.6 %copy-start = (bf16[320,4096]{1,0:T(8,128)(2,1)S(1)}, bf16[320,4096]{1,0:T(8,128)(2,1)}, u32[]{:S(2)}) copy-start(bf16[320,4096]{1,0:T(8,128)(2,1)} %param.12) | copy-start | bytes 7864324
  2.7 16.6 %copy-start.1 = (bf16[4096,320]{0,1:T(8,128)(2,1)S(1)}, bf16[4096,320]{0,1:T(8,128)(2,1)}, u32[]{:S(2)}) copy-start(bf16[4096,320]{0,1:T(8,128)(2,1)} %param.10) | copy-start | bytes 7864324
  20.2 8.2 %copy-start.2 = (s32[128,8]{0,1:T(8,128)S(1)}, s32[128,8]{0,1:T(8,128)}, u32[]{:S(2)}) copy-start(s32[128,8]{0,1:T(8,128)} %param.8) | copy-start | bytes 12292
  20.3 32.3 %copy-start.3 = (f32[128]{0:T(128)S(1)}, f32[128]{0:T(128)}, u32[]{:S(2)}) copy-start(f32[128]{0:T(128)} %param.13) | copy-start | bytes 1540
  25.0 28.1 %all-to-all-start.1 = ((bf16[4,16,4096]{2,1,0:T(8,128)(2,1)}), bf16[4,16,4096]{2,1,0:T(8,128)(2,1)S(1)}, u32[]{:S(2)}, u32[]{:S(2)}) async-start(bf16[4,16,4096]{2,1,0:T(8,128)(2,1)} %bitcast.18), calls=%async_computation.1 | async-start | bytes 1048576 | tf_op jit(solution)/shard_map/all_to_all | solution.py:50
  28.9 6.5 %collective-permute-start = (f32[128]{0:T(128)S(1)}, f32[128]{0:T(128)S(1)}, u32[]{:S(2)}, u32[]{:S(2)}) collective-permute-start(f32[128]{0:T(128)S(1)} %convert_reduce_fusion.1), channel_id=1, source_target_pairs={{0,8},{8,0},{16,24},{24,16},{1,9},{9,1},{17,25},{25,17},{2,10},{10... | collective-permute-start | bytes 1544 | tf_op jit(solution)/shard_map/ppermute | solution.py:18
  35.4 3.6 %collective-permute-start.1 = (f32[128]{0:T(128)S(1)}, f32[128]{0:T(128)S(1)}, u32[]{:S(2)}, u32[]{:S(2)}) collective-permute-start(f32[128]{0:T(128)S(1)} %add.30), channel_id=1, source_target_pairs={{0,16},{8,24},{16,0},{24,8},{1,17},{9,25},{17,1},{25,9},{2,18},{10... | collective-permute-start | bytes 1544 | tf_op jit(solution)/shard_map/ppermute | solution.py:18
